TPU v7x, 16 devices: a whole 2x2x2 slice. The times are simulated.
16 devices in a mesh: dp: 2 (over z), col: 2 (over y), row: 4 (over x, core).
Axes of the slice: x: 2, y: 2, z: 2, core: 2. Of those that a mesh axis runs over, the one named last changes fastest.
Arguments:
- x_attn: bfloat16 [16384, 1024], P('dp', 'row')
- dy_attn: bfloat16 [16384, 1024], P('dp', 'col')
- x_mlp: bfloat16 [16384, 1024], P('dp', 'row')
- dy_gate: bfloat16 [16384, 4096], P('dp', 'col')
- dy_up: bfloat16 [16384, 4096], P('dp', 'col')
- h_mlp: bfloat16 [16384, 4096], P('dp', 'row')
- dy_out: bfloat16 [16384, 1024], P('dp', 'col')
- w_attn: float32 [1024, 1024], P('row', 'col')
- w_gate: float32 [1024, 4096], P('row', 'col')
- w_up: float32 [1024, 4096], P('row', 'col')
- w_down: float32 [4096, 1024], P('row', 'col')
- r_attn: float32 [1024], P('row')
- c_attn: float32 [1024], P('col')
- r_gate: float32 [1024], P('row')
- c_gate: float32 [4096], P('col')
- r_up: float32 [1024], P('row')
- c_up: float32 [4096], P('col')
- r_down: float32 [4096], P('row')
- c_down: float32 [1024], P('col')
- hyper_params: float32 [3], replicated
Outputs:
- output 1: float32 [1024, 1024], P('row', 'col')
- output 2: float32 [1024], P('row')
- output 3: float32 [1024], P('col')
- output 4: float32 [1024, 4096], P('row', 'col')
- output 5: float32 [1024], P('row')
- output 6: float32 [4096], P('col')
- output 7: float32 [1024, 4096], P('row', 'col')
- output 8: float32 [1024], P('row')
- output 9: float32 [4096], P('col')
- output 10: float32 [4096, 1024], P('row', 'col')
- output 11: float32 [4096], P('row')
- output 12: float32 [1024], P('col')
All inputs are finite; a program needn't handle non-finite values.
Results may differ from a plain program's by a relative error of at most 0.001.
Values are sent between devices in bfloat16 or wider.
A program may use at most 1 GiB of HBM per device.

v0:
```python
import functools
import jax
import jax.numpy as jnp
from jax import lax
from jax.sharding import PartitionSpec as P

EPS_ONE = 1e-30
EPS_TWO = 1e-3


def matrix_step(x_block, dy_block, w_block, row_old, col_old, hyper_vals, row_size, col_size):
    beta_two = hyper_vals[0]
    rho_step = hyper_vals[1]
    clip_thr = hyper_vals[2]
    m_total = w_block.shape[0] * row_size
    n_total = w_block.shape[1] * col_size
    part_grad = jnp.einsum('tm,tn->mn', x_block, dy_block, preferred_element_type=jnp.float32)
    grad_block = lax.psum(part_grad, 'dp')
    sq_grad = grad_block * grad_block + EPS_ONE
    row_sum = lax.psum(jnp.sum(sq_grad, axis=1), 'col')
    col_sum = lax.psum(jnp.sum(sq_grad, axis=0), 'row')
    new_row = beta_two * row_old + (1.0 - beta_two) * (row_sum / n_total)
    new_col = beta_two * col_old + (1.0 - beta_two) * (col_sum / m_total)
    row_total = lax.psum(jnp.sum(new_row), 'row')
    second_est = new_row[:, None] * new_col[None, :] / row_total
    update = grad_block / jnp.sqrt(second_est)
    upd_rms = jnp.sqrt(lax.psum(jnp.sum(update * update), ('row', 'col')) / (m_total * n_total))
    update = update / jnp.maximum(1.0, upd_rms / clip_thr)
    w_rms = jnp.sqrt(lax.psum(jnp.sum(w_block * w_block), ('row', 'col')) / (m_total * n_total))
    step_size = rho_step * jnp.maximum(EPS_TWO, w_rms)
    return (w_block - step_size * update, new_row, new_col)


def solution(mesh):
    row_size = mesh.shape['row']
    col_size = mesh.shape['col']
    act_spec = P('dp', 'row')
    grad_spec = P('dp', 'col')
    w_spec = P('row', 'col')
    row_spec = P('row')
    col_spec = P('col')
    in_specs = (act_spec, grad_spec, act_spec, grad_spec, grad_spec, act_spec, grad_spec,
                w_spec, w_spec, w_spec, w_spec,
                row_spec, col_spec, row_spec, col_spec, row_spec, col_spec, row_spec, col_spec, P())
    out_specs = (w_spec, row_spec, col_spec) * 4

    def per_device(x_attn, dy_attn, x_mlp, dy_gate, dy_up, h_mlp, dy_out, w_attn, w_gate, w_up, w_down,
                   r_attn, c_attn, r_gate, c_gate, r_up, c_up, r_down, c_down, hyper_params):
        apply_one = functools.partial(matrix_step, hyper_vals=hyper_params, row_size=row_size, col_size=col_size)
        return (apply_one(x_attn, dy_attn, w_attn, r_attn, c_attn)
                + apply_one(x_mlp, dy_gate, w_gate, r_gate, c_gate)
                + apply_one(x_mlp, dy_up, w_up, r_up, c_up)
                + apply_one(h_mlp, dy_out, w_down, r_down, c_down))

    return jax.shard_map(per_device, mesh=mesh, in_specs=in_specs, out_specs=out_specs, check_vma=False)
```

profile of v0, /device:TPU:0, one launch (start us, length us, event | category | flops | bytes accessed | tf_op | source)
XLA Modules:
  0.0 304.4 jit_solution(8892976780657112405)
XLA Ops:
  7.2 17.4 %fusion.14 = f32[256,2048]{1,0:T(8,128)} fusion(bf16[8192,256]{1,0:T(8,128)(2,1)} %param.22, bf16[8192,2048]{1,0:T(8,128)(2,1)} %param.23), kind=kOutput, calls=%fused_computation.42 | convolution fusion | flops 8589934592 | bytes 39845888 | tf_op jit(solution)/shard_map/tm,tn->mn/dot_general | solution.py:17
  24.6 17.4 %fusion.15 = f32[256,2048]{1,0:T(8,128)} fusion(bf16[8192,256]{1,0:T(8,128)(2,1)} %param.22, bf16[8192,2048]{1,0:T(8,128)(2,1)} %param.24), kind=kOutput, calls=%fused_computation.43 | convolution fusion | flops 8589934592 | bytes 39845888 | tf_op jit(solution)/shard_map/tm,tn->mn/dot_general | solution.py:17
  42.0 15.9 %fusion.16 = f32[1024,512]{1,0:T(8,128)} fusion(bf16[8192,1024]{1,0:T(8,128)(2,1)} %param.25, bf16[8192,512]{1,0:T(8,128)(2,1)} %param.26), kind=kOutput, calls=%fused_computation.44 | convolution fusion | flops 8589934592 | bytes 27262976 | tf_op jit(solution)/shard_map/tm,tn->mn/dot_general | solution.py:17
  57.9 3.1 %fusion.13 = f32[256,512]{1,0:T(8,128)} fusion(bf16[8192,256]{1,0:T(8,128)(2,1)S(1)} %copy-done.6, bf16[8192,512]{1,0:T(8,128)(2,1)S(1)} %bitcast.12), kind=kOutput, calls=%fused_computation.41 | convolution fusion | flops 2147483648 | bytes 13107200 | tf_op jit(solution)/shard_map/tm,tn->mn/dot_general | solution.py:17
  63.9 1.1 multiply_reduce_fusion.1
  65.0 1.1 multiply_reduce_fusion.3
  66.2 1.1 multiply_reduce_fusion.5
  67.3 157.4 %all-reduce.6.cloned.1.call-done = (f32[256,512]{1,0:T(8,128)}, f32[256,2048]{1,0:T(8,128)}, f32[256,2048]{1,0:T(8,128)}, f32[1024,512]{1,0:T(8,128)}) async-done(((f32[256,512]{1,0:T(8,128)}, f32[256,2048]{1,0:T(8,128)}, f32[256,2048]{1,0:T(8,128)}, f32[1024,512]{1,0:T(8,128)}), (f32[256,512]{1,0:T(8,128)}, f32[256,2048]{1,0:T(8,128)}, f32[256,2048]{1,0:T(8,128)}, ...) | async-done | bytes 6815760 | tf_op jit(solution)/shard_map/psum | solution.py:18
  224.7 2.2 fusion.2
  228.3 5.0 %all-reduce.2 = (f32[256]{0:T(256)S(1)}, f32[256]{0:T(256)S(1)}, f32[256]{0:T(256)S(1)}, f32[1024]{0:T(1024)S(1)}) all-reduce(f32[256]{0:T(256)S(1)} %get-tuple-element.19, f32[256]{0:T(256)S(1)} %get-tuple-element.17, f32[256]{0:T(256)S(1)} %get-tuple-element.15, ...), channel_id=1, replica_groups=mesh['dp'=2,'col'=2,'row'=4] {'col'}, use_global_device_ids=true, to_apply=%region_4.0 | all-reduce | flops 1792 | bytes 14336 | tf_op jit(solution)/shard_map/psum | solution.py:20
  233.3 1.2 fusion.8
  234.5 1.2 fusion.11
  235.8 1.2 fusion.9
  237.0 1.2 fusion.10
  238.3 11.4 %all-reduce.1 = (f32[]{:T(128)}, f32[512]{0:T(512)S(1)}, f32[]{:T(128)}, f32[2048]{0:T(1024)S(1)}, f32[]{:T(128)}, /*index=5*/f32[2048]{0:T(1024)S(1)}, f32[]{:T(128)}, f32[512]{0:T(512)S(1)}) all-reduce(f32[]{:T(128)} %get-tuple-element.50, f32[512]{0:T(512)S(1)} %get-tuple-element.18, ...), channel_id=1, replica_groups=mesh['dp'=2,'col'=2,'row'=4] {'row'}, use_global_device_ids=true, to_apply=%region_8.0 | all-reduce | flops 5124 | bytes 40992 | tf_op jit(solution)/shard_map/psum | solution.py:24
  249.6 0.8 multiply_add_fusion.7
  252.5 2.2 multiply_reduce_fusion
  254.7 2.2 multiply_reduce_fusion.2
  257.0 2.1 multiply_reduce_fusion.4
  259.1 1.5 multiply_reduce_fusion.6
  260.6 14.0 %all-reduce = (f32[]{:T(128)}, f32[]{:T(128)}, f32[]{:T(128)}, f32[]{:T(128)}, f32[]{:T(128)}, /*index=5*/f32[]{:T(128)}, f32[]{:T(128)}, f32[]{:T(128)}) all-reduce(f32[]{:T(128)} %multiply_reduce_fusion.6, f32[]{:T(128)} %multiply_reduce_fusion.7, f32[]{:T(128)} %multiply_reduce_fusion.4, ...), channel_id=1, replica_groups=mesh['dp'=2,'col'=2,'row'=4] {'row','col'}, use_global_device_ids=true, to_apply=%region_10.0 | all-reduce | flops 8 | bytes 64 | tf_op jit(solution)/shard_map/psum | solution.py:27
  285.2 4.7 %multiply_subtract_fusion = f32[1024,512]{1,0:T(8,128)} fusion(f32[1024,512]{1,0:T(8,128)} %param.30, f32[]{:T(128)S(6)} %max.31, f32[]{:T(128)S(6)} %mul.261, f32[1024,512]{1,0:T(8,128)S(1)} %copy-done, f32[]{:T(128)} %get-tuple-element.34, f32[512]{0:T(512)S(1)} %multiply_add_fusion.7, f32[1024]{0:T(1024)S(1)} %get-tuple-element.45), kind=kLoop, calls=%fused_computation | loop fusion | flops 3145728 | bytes 6297612 | tf_op jit(solution)/shard_map/sub | solution.py:31
  289.8 1.6 multiply_subtract_fusion.3
  291.5 6.0 %multiply_subtract_fusion.1 = (f32[256,2048]{1,0:T(8,128)}, f32[256,2048]{1,0:T(8,128)}) fusion(f32[256,2048]{1,0:T(8,128)} %param.29, f32[]{:T(128)S(6)} %max.29, f32[]{:T(128)S(6)} %mul.248, f32[256,2048]{1,0:T(8,128)S(1)} %copy-done.5, f32[]{:T(128)} %get-tuple-element.32, f32[2048]{0:T(1024)S(1)} %multiply_add_fusion.4, f32[256]{0:T(256)S(1)} %get-tuple-element.47, ...), kind=kLoop, calls=%fused_computation.5 | loop fusion | flops 6291456 | bytes 12601368 | tf_op jit(solution)/shard_map/sub | solution.py:31
  (75 shorter events, 5.6 us)
Async XLA Ops:
  7.2 217.5 %all-reduce.6.cloned.1.call-start = ((), (), s32[]{:S(2)}) async-start(), calls=%async_computation | async-start | bytes 13631488 | tf_op jit(solution)/shard_map/psum | solution.py:18
  7.2 50.7 %slice-start = ((s8[8388608]{0:T(1024)(128)(4,1)}), s8[4194304]{0:T(1024)(128)(4,1)S(1)}, s32[]{:S(2)}) async-start(s8[8388608]{0:T(1024)(128)(4,1)} %bitcast.11), calls=%async_computation.1 | async-start | bytes 8388608
  24.6 33.3 %slice-start.1 = ((s8[8388608]{0:T(1024)(128)(4,1)}), s8[4194304]{0:T(1024)(128)(4,1)S(1)}, s32[]{:S(2)}) async-start(s8[8388608]{0:T(1024)(128)(4,1)} %bitcast.11), calls=%async_computation.2 | async-start | bytes 8388608
  42.0 15.9 %copy-start.6 = (bf16[8192,256]{1,0:T(8,128)(2,1)S(1)}, bf16[8192,256]{1,0:T(8,128)(2,1)}, u32[]{:S(2)}) copy-start(bf16[8192,256]{1,0:T(8,128)(2,1)} %param.20) | copy-start | bytes 12582916
  226.9 6.3 %copy-start.24 = (f32[1024]{0:T(1024)S(1)}, f32[1024]{0:T(1024)}, u32[]{:S(2)}) copy-start(f32[1024]{0:T(1024)} %param.37) | copy-start | bytes 12292
  226.9 7.6 %copy-start.27 = (f32[256]{0:T(256)S(1)}, f32[256]{0:T(256)}, u32[]{:S(2)}) copy-start(f32[256]{0:T(256)} %param.31) | copy-start | bytes 3076
  226.9 8.8 %copy-start.28 = (f32[256]{0:T(256)S(1)}, f32[256]{0:T(256)}, u32[]{:S(2)}) copy-start(f32[256]{0:T(256)} %param.35) | copy-start | bytes 3076
  226.9 10.1 %copy-start.29 = (f32[256]{0:T(256)S(1)}, f32[256]{0:T(256)}, u32[]{:S(2)}) copy-start(f32[256]{0:T(256)} %param.33) | copy-start | bytes 3076
  226.9 22.7 %copy-start.25 = (f32[512]{0:T(512)S(1)}, f32[512]{0:T(512)}, u32[]{:S(2)}) copy-start(f32[512]{0:T(512)} %param.38) | copy-start | bytes 6148
  227.0 23.5 %copy-start.21 = (f32[2048]{0:T(1024)S(1)}, f32[2048]{0:T(1024)}, u32[]{:S(2)}) copy-start(f32[2048]{0:T(1024)} %param.36) | copy-start | bytes 24580
  227.0 24.2 %copy-start.22 = (f32[2048]{0:T(1024)S(1)}, f32[2048]{0:T(1024)}, u32[]{:S(2)}) copy-start(f32[2048]{0:T(1024)} %param.34) | copy-start | bytes 24580
  227.0 24.8 %copy-start.26 = (f32[512]{0:T(512)S(1)}, f32[512]{0:T(512)}, u32[]{:S(2)}) copy-start(f32[512]{0:T(512)} %param.32) | copy-start | bytes 6148
  234.5 50.6 %copy-start.15 = (f32[1024]{0:T(1024)}, f32[1024]{0:T(1024)S(1)}, u32[]{:S(2)}) copy-start(f32[1024]{0:T(1024)S(1)} %get-tuple-element.45) | copy-start | bytes 12292
  235.8 54.1 %copy-start.20 = (f32[256]{0:T(256)}, f32[256]{0:T(256)S(1)}, u32[]{:S(2)}) copy-start(f32[256]{0:T(256)S(1)} %get-tuple-element.51) | copy-start | bytes 3076
  237.0 54.5 %copy-start.18 = (f32[256]{0:T(256)}, f32[256]{0:T(256)S(1)}, u32[]{:S(2)}) copy-start(f32[256]{0:T(256)S(1)} %get-tuple-element.47) | copy-start | bytes 3076
  238.3 53.2 %copy-start.19 = (f32[256]{0:T(256)}, f32[256]{0:T(256)S(1)}, u32[]{:S(2)}) copy-start(f32[256]{0:T(256)S(1)} %get-tuple-element.49) | copy-start | bytes 3076
  249.6 5.1 %copy-start.4 = (f32[256,2048]{1,0:T(8,128)S(1)}, f32[256,2048]{1,0:T(8,128)}, u32[]{:S(2)}) copy-start(f32[256,2048]{1,0:T(8,128)} %get-tuple-element.42) | copy-start | bytes 6291460
  250.4 34.7 %copy-start.16 = (f32[512]{0:T(512)}, f32[512]{0:T(512)S(1)}, u32[]{:S(2)}) copy-start(f32[512]{0:T(512)S(1)} %multiply_add_fusion.7) | copy-start | bytes 6148
  251.1 40.4 %copy-start.13 = (f32[2048]{0:T(1024)}, f32[2048]{0:T(1024)S(1)}, u32[]{:S(2)}) copy-start(f32[2048]{0:T(1024)S(1)} %multiply_add_fusion.4) | copy-start | bytes 24580
  251.8 39.7 %copy-start.14 = (f32[2048]{0:T(1024)}, f32[2048]{0:T(1024)S(1)}, u32[]{:S(2)}) copy-start(f32[2048]{0:T(1024)S(1)} %multiply_add_fusion.5) | copy-start | bytes 24580
  252.5 37.4 %copy-start.17 = (f32[512]{0:T(512)}, f32[512]{0:T(512)S(1)}, u32[]{:S(2)}) copy-start(f32[512]{0:T(512)S(1)} %multiply_add_fusion.8) | copy-start | bytes 6148
  285.1 6.4 %copy-start.3 = (f32[256,2048]{1,0:T(8,128)S(1)}, f32[256,2048]{1,0:T(8,128)}, u32[]{:S(2)}) copy-start(f32[256,2048]{1,0:T(8,128)} %get-tuple-element.41) | copy-start | bytes 6291460
  285.1 6.4 %copy-start.5 = (f32[256,2048]{1,0:T(8,128)S(1)}, f32[256,2048]{1,0:T(8,128)}, u32[]{:S(2)}) copy-start(f32[256,2048]{1,0:T(8,128)} %get-tuple-element.42) | copy-start | bytes 6291460
  285.1 6.4 %copy-start.9 = (f32[256,2048]{1,0:T(8,128)S(1)}, f32[256,2048]{1,0:T(8,128)}, u32[]{:S(2)}) copy-start(f32[256,2048]{1,0:T(8,128)} %param.28) | copy-start | bytes 6291460
  (9 other events, 20.4 us)
Sparse Core Ops, SparseCore 0:
  61.2 163.4 all-reduce.5
where the time goes:
time: 305 us; the launch traced here: 304 us
  waiting for transfers between devices  157 us (51%)
  matrix products  53.8 us (18%)
  other arithmetic  35.5 us (12%)
  blocking collectives  30.4 us (10%)
  between operations  25.4 us (8%)
    psum x1, waiting for transfers between devices, matrix_step(): grad_block = lax.psum(part_grad, 'dp')  157 us
    dot_general x4, matrix products, matrix_step(): jnp.einsum('tm,tn->mn', x_block, dy_block, preferred_element_type=jnp.flo...  53.8 us
    psum x1, blocking collectives, matrix_step(): lax.psum(jnp.sum(update * update), ('row', 'col')) / (m_total * n_total)  14 us
    sub x3, other arithmetic, matrix_step(): return (w_block - step_size * update, new_row, new_col)  12.3 us
    psum x1, blocking collectives, matrix_step(): row_total = lax.psum(jnp.sum(new_row), 'row')  11.4 us
    reduce_sum x4, other arithmetic, matrix_step(): jnp.sum(update * update)  8.09 us
  transfers between devices with their start and end apart: 1, of which 1 were waited for; matrix products, arithmetic and copies ran while one was open for 2% of the time, Pallas kernels for 0%

commit v1 on v0

v1 whole, which is shorter than its diff:
```python
import functools
import math

import jax
import jax.numpy as jnp
from jax import lax
from jax.experimental import pallas as pl
from jax.experimental.pallas import tpu as pltpu
from jax.sharding import PartitionSpec as P

EPS_ONE = 1e-30
EPS_TWO = 1e-3
MESH = pl.DeviceIdType.MESH
F32 = jnp.float32

TM, TN = 256, 512
KC = 1024
NB = 8
RB = 32
LANES = 128


def fold_lanes(v):
    total = v[:, :LANES]
    for j in range(LANES, v.shape[1], LANES):
        total = total + v[:, j:j + LANES]
    return total


def fold_rows(v):
    total = v[:8]
    for i in range(8, v.shape[0], 8):
        total = total + v[i:i + 8]
    return total


def kernel(geo, x_refs, dy_refs, w_refs, r_refs, c_refs, hyper, w_outs, r_outs, c_outs,
           xbuf, ybuf, part, peer, rowpart, acol, brow, msg_one, msg_two,
           x_sem, y_sem, w_sem, bulk_send, bulk_recv, one_send, one_recv, two_send, two_recv):
    n_col, n_row, n_chunk = geo.n_col, geo.n_row, geo.n_chunk
    plane = n_col * n_row
    dp, col, row = lax.axis_index("dp"), lax.axis_index("col"), lax.axis_index("row")
    me = col * n_row + row

    def plane_peer(step):
        other = lax.rem(me + step, plane)
        return other, (dp, lax.div(other, n_row), lax.rem(other, n_row))

    across = (1 - dp, col, row)

    def load(tile, k, slot):
        rows = pl.ds(pl.multiple_of(k * KC, KC), KC)
        for first, count, m_tiles, x_ref, y_ref in geo.groups(x_refs, dy_refs):
            @pl.when(jnp.logical_and(tile >= first, tile < first + count))
            def _():
                local = tile - first
                m_at = local if m_tiles > 1 else 0
                n_at = 0 if m_tiles > 1 else local
                pltpu.make_async_copy(
                    x_ref.at[rows, pl.ds(pl.multiple_of(m_at * TM, TM), TM)], xbuf.at[slot], x_sem.at[slot]).start()
                pltpu.make_async_copy(
                    y_ref.at[rows, pl.ds(pl.multiple_of(n_at * TN, TN), TN)], ybuf.at[slot], y_sem.at[slot]).start()

    def load_done(slot):
        pltpu.make_async_copy(x_refs[0].at[pl.ds(0, KC), pl.ds(0, TM)], xbuf.at[slot], x_sem.at[slot]).wait()
        pltpu.make_async_copy(dy_refs[0].at[pl.ds(0, KC), pl.ds(0, TN)], ybuf.at[slot], y_sem.at[slot]).wait()

    total_chunks = geo.n_tiles * n_chunk
    for c in range(NB - 1):
        load(c // n_chunk, c % n_chunk, c)

    barrier = pltpu.get_barrier_semaphore()
    for step in range(1, plane):
        pl.semaphore_signal(barrier, inc=1, device_id=plane_peer(step)[1], device_id_type=MESH)
    pl.semaphore_signal(barrier, inc=1, device_id=across, device_id_type=MESH)
    w_copies = [pltpu.make_async_copy(w_refs[i], w_outs[i], w_sem.at[i]) for i in range(4)]

    def bulk(tile):
        return pltpu.make_async_remote_copy(
            src_ref=part.at[tile], dst_ref=peer.at[tile], send_sem=bulk_send.at[tile], recv_sem=bulk_recv.at[tile],
            device_id=across, device_id_type=MESH)

    @pl.loop(0, geo.n_tiles)
    def _(tile):
        part[tile] = jnp.zeros((TM, TN), F32)

        @pl.loop(0, n_chunk)
        def _(k):
            chunk = tile * n_chunk + k
            slot = lax.rem(chunk, NB)
            load_done(slot)
            later = chunk + (NB - 1)

            @pl.when(later < total_chunks)
            def _():
                load(lax.div(later, n_chunk), lax.rem(later, n_chunk), lax.rem(later, NB))

            part[tile] += lax.dot_general(
                xbuf[slot], ybuf[slot], (((0,), (0,)), ((), ())), preferred_element_type=F32)

        @pl.when(tile == 0)
        def _():
            pl.semaphore_wait(barrier, plane)
            for copy in w_copies:
                copy.start()

        bulk(tile).start()

    for copy in w_copies:
        copy.wait()

    beta_two, rho_step, clip_thr = hyper[0], hyper[1], hyper[2]

    for i in range(4):
        first, count, m_loc, n_loc = geo.mats[i]
        wide = m_loc == TM
        one, two = msg_one[i], msg_two
        w_out = w_outs[i]
        w_at = (lambda t, r: (pl.ds(r, RB), pl.ds(t * TN, TN))) if wide else (lambda t, r: (pl.ds(t * TM + r, RB), pl.ds(0, TN)))
        stat_at = (lambda t, r: pl.ds(r, RB)) if wide else (lambda t, r: pl.ds(t * TM + r, RB))
        col_at = m_loc

        if wide:
            rowpart[pl.ds(0, TM), :] = jnp.zeros((TM, LANES), F32)
        w_sq = jnp.zeros((8, LANES), F32)
        col_sum = jnp.zeros((8, TN), F32)
        for t in range(count):
            bulk(first + t).wait_recv()

            def stat_pass(b, carry):
                c_acc, w_acc = carry
                r = pl.multiple_of(b * RB, RB)
                grad = part[first + t, pl.ds(r, RB), :] + peer[first + t, pl.ds(r, RB), :]
                peer[first + t, pl.ds(r, RB), :] = grad
                sq = grad * grad + EPS_ONE
                folded = fold_lanes(sq)
                at = stat_at(t, r)
                if wide:
                    rowpart[at, :] += folded
                else:
                    rowpart[at, :] = folded
                w = w_out[w_at(t, r)]
                return c_acc + fold_rows(sq), w_acc + fold_rows(fold_lanes(w * w))

            col_sum, w_sq = lax.fori_loop(0, TM // RB, stat_pass, (col_sum, w_sq))
            if wide:
                one[pl.ds(me, 1), :, pl.ds(col_at + t * TN, TN)] = jnp.sum(col_sum, axis=0, keepdims=True)[None]
                col_sum = jnp.zeros((8, TN), F32)
        if not wide:
            one[pl.ds(me, 1), :, pl.ds(col_at, TN)] = jnp.sum(col_sum, axis=0, keepdims=True)[None]
        r_fold = jnp.zeros((1, LANES), F32)
        for j in range(0, m_loc, LANES):
            turned = jnp.transpose(rowpart[pl.ds(j, LANES), :])
            one[pl.ds(me, 1), :, pl.ds(j, LANES)] = jnp.sum(turned, axis=0, keepdims=True)[None]
            r_fold = r_fold + r_refs[i][:, pl.ds(j, LANES)]
        tail = m_loc + n_loc
        one[pl.ds(me, 1), :, pl.ds(tail, LANES)] = r_fold[None]
        one[pl.ds(me, 1), :, pl.ds(tail + LANES, LANES)] = jnp.sum(w_sq, axis=0, keepdims=True)[None]

        def exchange(buf, send, recv):
            copies = []
            for step in range(1, plane):
                _, device = plane_peer(step)
                copies.append(pltpu.make_async_remote_copy(
                    src_ref=buf.at[me], dst_ref=buf.at[me], send_sem=send.at[i, step], recv_sem=recv.at[i, me],
                    device_id=device, device_id_type=MESH))
            for copy in copies:
                copy.start()
            for step in range(1, plane):
                other, device = plane_peer(step)
                pltpu.make_async_remote_copy(
                    src_ref=buf.at[other], dst_ref=buf.at[other], send_sem=send.at[i, step], recv_sem=recv.at[i, other],
                    device_id=device, device_id_type=MESH).wait_recv()
            return copies

        sent = exchange(one, one_send, one_recv)

        m_total, n_total = m_loc * n_row, n_loc * n_col
        row_sum = one[row, :, pl.ds(0, m_loc)]
        for j in range(1, n_col):
            row_sum = row_sum + one[j * n_row + row, :, pl.ds(0, m_loc)]
        cols = [one[col * n_row + j, :, pl.ds(m_loc, n_loc)] for j in range(n_row)]
        while len(cols) > 1:
            cols = [cols[j] + cols[j + 1] for j in range(0, len(cols), 2)]
        new_row = beta_two * r_refs[i][...] + (1.0 - beta_two) * (row_sum / n_total)
        new_col = beta_two * c_refs[i][...] + (1.0 - beta_two) * (cols[0] / m_total)
        r_outs[i][...] = new_row
        c_outs[i][...] = new_col

        old_fold = jnp.zeros((1, LANES), F32)
        sq_fold = jnp.zeros((1, LANES), F32)
        w_fold = jnp.zeros((1, LANES), F32)
        for j in range(plane):
            sq_fold = sq_fold + fold_lanes(one[j, :, pl.ds(0, m_loc)])
            w_fold = w_fold + one[j, :, pl.ds(tail + LANES, LANES)]
            if j < n_row:
                old_fold = old_fold + one[j, :, pl.ds(tail, LANES)]
        row_total = jnp.sum(beta_two * old_fold + (1.0 - beta_two) * (sq_fold / n_total), axis=1, keepdims=True)
        w_rms = jnp.sqrt(jnp.sum(w_fold, axis=1, keepdims=True) / (m_total * n_total))

        row_scale = 1.0 / jnp.sqrt(new_row / row_total)
        col_scale = 1.0 / jnp.sqrt(new_col)
        for j in range(0, m_loc, LANES):
            spread = jnp.broadcast_to(row_scale[:, j:j + LANES], (LANES, LANES))
            acol[pl.ds(j, LANES), :] = jnp.transpose(spread)
        brow[:, pl.ds(0, n_loc)] = col_scale

        upd_sq = jnp.zeros((8, LANES), F32)
        for t in range(count):
            scale = brow[:, pl.ds(t * TN if wide else 0, TN)]

            def norm_pass(b, acc):
                r = pl.multiple_of(b * RB, RB)
                upd = peer[first + t, pl.ds(r, RB), :] * scale
                lane_scale = acol[stat_at(t, r), :]
                return acc + fold_rows(fold_lanes(upd * upd) * lane_scale * lane_scale)

            upd_sq = lax.fori_loop(0, TM // RB, norm_pass, upd_sq)
        two_i = two.at[i]
        two_i[pl.ds(me, 1)] = jnp.sum(upd_sq, axis=0, keepdims=True)[None]
        sent += exchange(two_i, two_send, two_recv)
        upd_fold = two_i[0]
        for j in range(1, plane):
            upd_fold = upd_fold + two_i[j]
        upd_rms = jnp.sqrt(jnp.sum(upd_fold, axis=1, keepdims=True) / (m_total * n_total))
        step_size = rho_step * jnp.maximum(EPS_TWO, w_rms) / jnp.maximum(1.0, upd_rms / clip_thr)
        brow[:, pl.ds(0, n_loc)] = col_scale * step_size
        for t in range(count):
            scale = brow[:, pl.ds(t * TN if wide else 0, TN)]

            def write_pass(b, _):
                r = pl.multiple_of(b * RB, RB)
                upd = peer[first + t, pl.ds(r, RB), :] * scale
                lane_scale = acol[stat_at(t, r), :]
                wide_scale = jnp.concatenate([lane_scale] * (TN // LANES), axis=1)
                w_out[w_at(t, r)] = w_out[w_at(t, r)] - upd * wide_scale
                return 0

            lax.fori_loop(0, TM // RB, write_pass, 0)
        for copy in sent:
            copy.wait_send()

    @pl.loop(0, geo.n_tiles)
    def _(tile):
        bulk(tile).wait_send()


class Geometry:
    def __init__(self, n_row, n_col, tokens, blocks):
        self.n_row, self.n_col = n_row, n_col
        self.n_chunk = tokens // KC
        self.mats, first = [], 0
        for m_loc, n_loc in blocks:
            count = (m_loc // TM) * (n_loc // TN)
            self.mats.append((first, count, m_loc, n_loc))
            first += count
        self.n_tiles = first

    def groups(self, x_refs, dy_refs):
        for (first, count, m_loc, _), x_ref, y_ref in zip(self.mats, x_refs, dy_refs):
            yield first, count, m_loc // TM, x_ref, y_ref


def solution(mesh):
    n_row, n_col = mesh.shape["row"], mesh.shape["col"]
    plane = n_row * n_col
    act_spec = P('dp', 'row')
    grad_spec = P('dp', 'col')
    w_spec = P('row', 'col')
    row_spec = P('row')
    col_spec = P('col')
    in_specs = (act_spec, grad_spec, act_spec, grad_spec, grad_spec, act_spec, grad_spec,
                w_spec, w_spec, w_spec, w_spec,
                row_spec, col_spec, row_spec, col_spec, row_spec, col_spec, row_spec, col_spec, P())
    out_specs = (w_spec, row_spec, col_spec) * 4

    def per_device(x_attn, dy_attn, x_mlp, dy_gate, dy_up, h_mlp, dy_out, w_attn, w_gate, w_up, w_down,
                   r_attn, c_attn, r_gate, c_gate, r_up, c_up, r_down, c_down, hyper_params):
        weights = (w_gate, w_up, w_down, w_attn)
        rows = [v.reshape(1, -1) for v in (r_gate, r_up, r_down, r_attn)]
        cols = [v.reshape(1, -1) for v in (c_gate, c_up, c_down, c_attn)]
        blocks = [w.shape for w in weights]
        geo = Geometry(n_row, n_col, x_attn.shape[0], blocks)
        hbm = pl.BlockSpec(memory_space=pl.ANY)
        vmem = pl.BlockSpec(memory_space=pltpu.VMEM)
        smem = pl.BlockSpec(memory_space=pltpu.SMEM)
        dma = pltpu.SemaphoreType.DMA
        max_m, max_n = max(b[0] for b in blocks), max(b[1] for b in blocks)

        def body(*refs):
            xs = (refs[0], refs[0], refs[1], refs[2])
            kernel(geo, xs, refs[3:7], refs[7:11], refs[11:15], refs[15:19], refs[19],
                   refs[20:24], refs[24:28], refs[28:32],
                   *refs[32:39], refs[39:43], *refs[43:])

        outs = pl.pallas_call(
            body,
            out_shape=tuple(pltpu.VMEM(w.shape, F32) for w in weights)
            + tuple(jax.ShapeDtypeStruct(v.shape, F32) for v in rows)
            + tuple(jax.ShapeDtypeStruct(v.shape, F32) for v in cols),
            in_specs=[hbm] * 3 + [hbm] * 4 + [hbm] * 4 + [vmem] * 8 + [smem],
            out_specs=(vmem,) * 12,
            scratch_shapes=[
                pltpu.VMEM((NB, KC, TM), jnp.bfloat16),
                pltpu.VMEM((NB, KC, TN), jnp.bfloat16),
                pltpu.VMEM((geo.n_tiles, TM, TN), F32),
                pltpu.VMEM((geo.n_tiles, TM, TN), F32),
                pltpu.VMEM((max_m, LANES), F32),
                pltpu.VMEM((max_m, LANES), F32),
                pltpu.VMEM((1, max_n), F32),
            ] + [pltpu.VMEM((plane, 1, m + n + 2 * LANES), F32) for m, n in blocks] + [
                pltpu.VMEM((4, plane, 1, LANES), F32),
                dma((NB,)), dma((NB,)), dma((4,)),
                dma((geo.n_tiles,)), dma((geo.n_tiles,)),
                dma((4, plane)), dma((4, plane)), dma((4, plane)), dma((4, plane)),
            ],
            compiler_params=pltpu.CompilerParams(
                collective_id=0, has_side_effects=True, vmem_limit_bytes=48 << 20),
            name="adafactor_step",
        )(x_mlp, h_mlp, x_attn, dy_gate, dy_up, dy_out, dy_attn, *weights, *rows, *cols, hyper_params)
        w_new, r_new, c_new = outs[:4], outs[4:8], outs[8:]
        result = []
        for i in (3, 0, 1, 2):
            result += [w_new[i], r_new[i].reshape(-1), c_new[i].reshape(-1)]
        return tuple(result)

    return jax.shard_map(per_device, mesh=mesh, in_specs=in_specs, out_specs=out_specs, check_vma=False)
```

time: 305 us -> 176 us (0.58)
  Pallas kernels: 0 us -> 166 us
  waiting for transfers between devices: 157 us -> 0 us
  matrix products: 53.8 us -> 0 us
  other arithmetic: 35.5 us -> 0 us
  blocking collectives: 30.4 us -> 0 us
  between operations: 25.4 us -> 0.71 us
  local copies, waits for them, and re-layouts: 1.79 us -> 9.43 us
    pallas_call x0 -> x1, Pallas kernels: none -> 166 us  [per_device(): pl.pallas_call(body, out_shape=tuple((pltpu.VMEM(w.shape, F32) for w in w...]
    psum x1 -> x0, waiting for transfers between devices: 157 us -> none  [matrix_step(): grad_block = lax.psum(part_grad, 'dp')]
    dot_general x4 -> x0, matrix products: 53.8 us -> none  [matrix_step(): jnp.einsum('tm,tn->mn', x_block, dy_block, preferred_element_type=jnp.flo...]
    psum x3 -> x0, blocking collectives: 30.4 us -> none  [the longest x1 14 us: matrix_step(): lax.psum(jnp.sum(update * update), ('row', 'col')) / (m_total * n_total)]
    reduce_sum x16 -> x0, other arithmetic: 20.4 us -> none  [the longest x4 8.09 us: matrix_step(): jnp.sum(update * update)]
    sub x3 -> x0, other arithmetic: 12.3 us -> none  [matrix_step(): return (w_block - step_size * update, new_row, new_col)]
    unnamed x64 -> x28, local copies, waits for them, and re-layouts: 1.12 us -> 9.43 us
  transfers between devices with their start and end apart: 1 -> 0, of which waited for: 1 -> 0; matrix products, arithmetic and copies ran while one was open for 2% -> 0% of each run, Pallas kernels for 0% -> 0%
where the time goes in v1:
time: 176 us
  Pallas kernels  166 us (94%)
  local copies, waits for them, and re-layouts  9.43 us (5%)
    pallas_call x1, Pallas kernels, per_device(): pl.pallas_call(body, out_shape=tuple((pltpu.VMEM(w.shape, F32) for w in w...  166 us
    unnamed x28, local copies, waits for them, and re-layouts  9.43 us

profile of v1, /device:TPU:0, one launch (start us, length us, event | category | flops | bytes accessed | tf_op | source)
XLA Modules:
  0.0 175.8 jit_solution(7220985581803553548)
XLA Ops:
  0.7 165.6 %adafactor_step.1 = (f32[256,2048]{1,0:T(8,128)S(1)}, f32[256,2048]{1,0:T(8,128)S(1)}, f32[1024,512]{1,0:T(8,128)S(1)}, f32[256,512]{1,0:T(8,128)S(1)}, f32[1,25...) custom-call(bf16[8192,256]{1,0:T(8,128)(2,1)} %refs_0_.1, ...), custom_call_target="tpu_custom_call" | custom-call | tf_op jit(solution)/shard_map/adafactor_step/pallas_call | solution.py:296
  166.3 0.8 copy.44
  167.1 1.3 copy.45
  168.4 1.3 copy.46
  169.7 0.0 copy-start.5
  169.7 0.0 copy-start
  169.7 0.0 copy-start.2
  169.8 0.0 copy-start.3
  169.8 1.3 copy.47
  171.1 0.0 copy-done.7
  171.1 0.6 copy.48
  171.7 0.0 copy-done.4
  171.7 0.6 copy.49
  172.2 0.0 copy-done.6
  172.2 0.6 copy.50
  172.8 0.0 copy-done.1
  172.8 0.6 copy.51
  173.4 0.0 copy-done.5
  173.4 0.6 copy.52
  174.0 0.0 copy-done
  174.0 0.6 copy.53
  174.6 0.0 copy-done.2
  174.6 0.6 copy.54
  175.2 0.6 copy.55
  (5 shorter events, 0.0 us)
Async XLA Ops:
  169.7 1.4 copy-start.7
  169.7 1.9 %copy-start.4 = (f32[1,512]{1,0:T(1,128)S(1)}, f32[1,512]{1,0:T(1,128)}, u32[]{:S(2)}) copy-start(f32[1,512]{1,0:T(1,128)} %get-tuple-element.26) | copy-start | bytes 6148
  169.7 2.5 %copy-start.6 = (f32[1,256]{1,0:T(1,128)S(1)}, f32[1,256]{1,0:T(1,128)}, u32[]{:S(2)}) copy-start(f32[1,256]{1,0:T(1,128)} %get-tuple-element.28) | copy-start | bytes 3076
  169.7 3.1 %copy-start.1 = (f32[1,2048]{1,0:T(1,128)S(1)}, f32[1,2048]{1,0:T(1,128)}, u32[]{:S(2)}) copy-start(f32[1,2048]{1,0:T(1,128)} %get-tuple-element.29) | copy-start | bytes 24580
  169.7 3.7 %copy-start.5 = (f32[1,256]{1,0:T(1,128)S(1)}, f32[1,256]{1,0:T(1,128)}, u32[]{:S(2)}) copy-start(f32[1,256]{1,0:T(1,128)} %get-tuple-element.31) | copy-start | bytes 3076
  169.7 4.2 %copy-start = (f32[1,2048]{1,0:T(1,128)S(1)}, f32[1,2048]{1,0:T(1,128)}, u32[]{:S(2)}) copy-start(f32[1,2048]{1,0:T(1,128)} %get-tuple-element.32) | copy-start | bytes 24580
  169.7 4.8 %copy-start.2 = (f32[1,1024]{1,0:T(1,128)S(1)}, f32[1,1024]{1,0:T(1,128)}, u32[]{:S(2)}) copy-start(f32[1,1024]{1,0:T(1,128)} %get-tuple-element.34) | copy-start | bytes 12292
  169.8 5.4 %copy-start.3 = (f32[1,512]{1,0:T(1,128)S(1)}, f32[1,512]{1,0:T(1,128)}, u32[]{:S(2)}) copy-start(f32[1,512]{1,0:T(1,128)} %get-tuple-element.35) | copy-start | bytes 6148

commit v2 on v1

--- a/solution.py
+++ b/solution.py
@@ -245,6 +245,14 @@
         bulk(tile).wait_send()
 
 
+def write_out(*refs):
+    copies = [pltpu.make_async_copy(refs[i], refs[12 + i], refs[24].at[i]) for i in range(12)]
+    for copy in copies:
+        copy.start()
+    for copy in copies:
+        copy.wait()
+
+
 class Geometry:
     def __init__(self, n_row, n_col, tokens, blocks):
         self.n_row, self.n_col = n_row, n_col
@@ -281,6 +289,7 @@
         cols = [v.reshape(1, -1) for v in (c_gate, c_up, c_down, c_attn)]
         blocks = [w.shape for w in weights]
         geo = Geometry(n_row, n_col, x_attn.shape[0], blocks)
+        results = (*weights, *rows, *cols)
         hbm = pl.BlockSpec(memory_space=pl.ANY)
         vmem = pl.BlockSpec(memory_space=pltpu.VMEM)
         smem = pl.BlockSpec(memory_space=pltpu.SMEM)
@@ -295,9 +304,7 @@
 
         outs = pl.pallas_call(
             body,
-            out_shape=tuple(pltpu.VMEM(w.shape, F32) for w in weights)
-            + tuple(jax.ShapeDtypeStruct(v.shape, F32) for v in rows)
-            + tuple(jax.ShapeDtypeStruct(v.shape, F32) for v in cols),
+            out_shape=tuple(pltpu.VMEM(v.shape, F32) for v in results),
             in_specs=[hbm] * 3 + [hbm] * 4 + [hbm] * 4 + [vmem] * 8 + [smem],
             out_specs=(vmem,) * 12,
             scratch_shapes=[
@@ -318,6 +325,14 @@
                 collective_id=0, has_side_effects=True, vmem_limit_bytes=48 << 20),
             name="adafactor_step",
         )(x_mlp, h_mlp, x_attn, dy_gate, dy_up, dy_out, dy_attn, *weights, *rows, *cols, hyper_params)
+        outs = pl.pallas_call(
+            write_out,
+            out_shape=tuple(jax.ShapeDtypeStruct(v.shape, F32) for v in results),
+            in_specs=[vmem] * 12,
+            out_specs=(hbm,) * 12,
+            scratch_shapes=[dma((12,))],
+            name="write_out", compiler_params=pltpu.CompilerParams(vmem_limit_bytes=1 << 20),
+        )(*[pltpu.with_memory_space_constraint(v, pltpu.VMEM) for v in outs])
         w_new, r_new, c_new = outs[:4], outs[4:8], outs[8:]
         result = []
         for i in (3, 0, 1, 2):

time: 176 us -> 169 us (0.960)
  local copies, waits for them, and re-layouts: 9.43 us -> 0 us
  Pallas kernels: 166 us -> 168 us
    unnamed x28 -> x0, local copies, waits for them, and re-layouts: 9.43 us -> none
    pallas_call x1 -> x2, Pallas kernels: 166 us -> 168 us  [the longest x1 165 us: per_device(): pl.pallas_call(body, out_shape=tuple((pltpu.VMEM(v.shape, F32) for v in r...]
where the time goes in v2:
time: 169 us
  Pallas kernels  168 us (99%)
    pallas_call x1, Pallas kernels, per_device(): pl.pallas_call(body, out_shape=tuple((pltpu.VMEM(v.shape, F32) for v in r...  165 us

profile of v2, /device:TPU:0, one launch (start us, length us, event | category | flops | bytes accessed | tf_op | source)
XLA Modules:
  0.0 168.6 jit_solution(8533273565851412041)
XLA Ops:
  0.7 165.0 %adafactor_step.1 = (f32[256,2048]{1,0:T(8,128)S(1)}, f32[256,2048]{1,0:T(8,128)S(1)}, f32[1024,512]{1,0:T(8,128)S(1)}, f32[256,512]{1,0:T(8,128)S(1)}, f32[1,25...) custom-call(bf16[8192,256]{1,0:T(8,128)(2,1)} %refs_0_.1, ...), custom_call_target="tpu_custom_call" | custom-call | tf_op jit(solution)/shard_map/adafactor_step/pallas_call | solution.py:305
  165.6 2.9 %write_out.1 = (f32[256,2048]{1,0:T(8,128)}, f32[256,2048]{1,0:T(8,128)}, f32[1024,512]{1,0:T(8,128)}, f32[256,512]{1,0:T(8,128)}, f32[1,256]{1,0:T(1,128)}, /*i...) custom-call(f32[256,2048]{1,0:T(8,128)S(1)} %get-tuple-element.36.re, ...), custom_call_target="tpu_custom_call" | custom-call | tf_op jit(solution)/shard_map/write_out/pallas_call | solution.py:328

commit v3 on v2

v3 whole, which is shorter than its diff:
```python
import jax
import jax.numpy as jnp
from jax import lax
from jax.experimental import pallas as pl
from jax.experimental.pallas import tpu as pltpu
from jax.sharding import PartitionSpec as P

EPS_ONE = 1e-30
EPS_TWO = 1e-3
MESH = pl.DeviceIdType.MESH
F32 = jnp.float32

TM, TN = 256, 512
HALVES = 2
PARTS = ((0, 128, 0, 128), (128, 128, 0, 128), (0, 256, 128, 128), (0, 256, 256, 256))
RB = 32
LANES = 128


def fold_lanes(v):
    total = v[:, :LANES]
    for j in range(LANES, v.shape[1], LANES):
        total = total + v[:, j:j + LANES]
    return total


def fold_rows(v):
    total = v[:8]
    for i in range(8, v.shape[0], 8):
        total = total + v[i:i + 8]
    return total


def lane_sum(v):
    return jnp.sum(v, axis=1, keepdims=True)


def row_sum_of(v):
    return jnp.sum(v, axis=0, keepdims=True)


def kernel(geo, x_refs, dy_refs, w_refs, r_refs, c_refs, hyper, w_outs, r_outs, c_outs,
           xbuf, ybuf, part, peer, rowpart, rowpart_own, acol, brow, colpart, w_sq, msg_one, msg_two, zmsg_one, zmsg_two,
           x_sem, y_sem, first_sem, w_sem, sub_send, sub_recv, bulk_send, bulk_recv, gather_sem,
           one_send, one_recv, two_send, two_recv, z_send, z_recv):
    n_col, n_row = geo.n_col, geo.n_row
    plane = n_col * n_row
    dp, col, row = lax.axis_index("dp"), lax.axis_index("col"), lax.axis_index("row")
    me = col * n_row + row
    own, other = dp, 1 - dp
    across = (1 - dp, col, row)

    def plane_peer(step):
        other = lax.rem(me + step, plane)
        return other, (dp, lax.div(other, n_row), lax.rem(other, n_row))

    def remote(src, dst, send, recv, device):
        return pltpu.make_async_remote_copy(
            src_ref=src, dst_ref=dst, send_sem=send, recv_sem=recv, device_id=device, device_id_type=MESH)

    def first_part(tile, j):
        r0, r_n, c0, c_n = PARTS[j]
        at = (tile, pl.ds(r0, r_n), pl.ds(c0, c_n))
        return remote(part.at[at], peer.at[at], sub_send.at[j], sub_recv.at[j], across)

    def bulk(tile):
        return remote(part.at[tile], peer.at[tile], bulk_send.at[tile], bulk_recv.at[tile], across)

    def gather(tile):
        at = (slice(None), pl.ds(pl.multiple_of(tile * TN, TN), TN))
        return remote(w_outs[0].at[at], w_outs[0].at[at], gather_sem.at[0], gather_sem.at[1], across)

    def z_copy(n, buf, slot):
        return remote(buf.at[slot], buf.at[slot], z_send.at[n], z_recv.at[n], across)

    half = geo.tokens // HALVES

    def first_x(n, pieces, c, c0, c_n):
        rows = pl.ds(c * (geo.tokens // pieces), geo.tokens // pieces)
        at = (rows, pl.ds(c0, c_n))
        return pltpu.make_async_copy(x_refs[0].at[at], xbuf.at[0].at[at], first_sem.at[n, c])

    def first_y(n, pieces, c, c0, c_n):
        rows = pl.ds(c * (geo.tokens // pieces), geo.tokens // pieces)
        columns = pl.ds(pl.multiple_of(other * TN + c0, LANES), c_n)
        return pltpu.make_async_copy(dy_refs[0].at[rows, columns], ybuf.at[0, rows, pl.ds(c0, c_n)], first_sem.at[n, c])

    n_steps = geo.n_tiles - 1

    def tile_of(s):
        past_zero = lax.div(s + (n_steps - 1), n_steps)
        past_one = lax.div(s + (n_steps - 2), n_steps)
        return s + 1 + (1 - past_zero) - (past_zero - past_one) * (2 - own)

    def slot_of(s):
        return lax.rem(s + 1, 2)

    def load(s):
        tile, slot = tile_of(s), slot_of(s)
        for first, count, m_tiles, x_ref, y_ref in geo.groups(x_refs, dy_refs):
            @pl.when(jnp.logical_and(tile >= first, tile < first + count))
            def _():
                local = tile - first
                m_at = local if m_tiles > 1 else 0
                n_at = 0 if m_tiles > 1 else local
                for h in range(HALVES):
                    rows = pl.ds(h * half, half)
                    pltpu.make_async_copy(
                        x_ref.at[rows, pl.ds(pl.multiple_of(m_at * TM, TM), TM)],
                        xbuf.at[slot, rows], x_sem.at[slot, h]).start()
                    pltpu.make_async_copy(
                        y_ref.at[rows, pl.ds(pl.multiple_of(n_at * TN, TN), TN)],
                        ybuf.at[slot, rows], y_sem.at[slot, h]).start()

    def load_done(slot, h):
        rows = pl.ds(h * half, half)
        pltpu.make_async_copy(x_refs[0].at[rows, pl.ds(0, TM)], xbuf.at[slot, rows], x_sem.at[slot, h]).wait()
        pltpu.make_async_copy(dy_refs[0].at[rows, pl.ds(0, TN)], ybuf.at[slot, rows], y_sem.at[slot, h]).wait()

    def contract(x, y):
        return lax.dot_general(x, y, (((0,), (0,)), ((), ())), preferred_element_type=F32)

    first_loads = (
        (4, lambda c: (first_x(0, 4, c, 0, 128), first_y(1, 4, c, 0, 128))),
        (2, lambda c: (first_x(2, 2, c, 128, 128),)),
        (2, lambda c: (first_y(3, 2, c, 128, 128),)),
        (2, lambda c: (first_y(4, 2, c, 256, 256),)),
    )
    for pieces, copies_of in first_loads:
        for c in range(pieces):
            for copy in copies_of(c):
                copy.start()
    load(0)

    barrier = pltpu.get_barrier_semaphore()
    for step in range(1, plane):
        pl.semaphore_signal(barrier, inc=1, device_id=plane_peer(step)[1], device_id_type=MESH)
    pl.semaphore_signal(barrier, inc=1, device_id=across, device_id_type=MESH)

    for j, (pieces, copies_of) in enumerate(first_loads):
        r0, r_n, c0, c_n = PARTS[j]
        at = (other, pl.ds(r0, r_n), pl.ds(c0, c_n))
        for c in range(pieces):
            for copy in copies_of(c):
                copy.wait()
            rows = pl.ds(c * (geo.tokens // pieces), geo.tokens // pieces)
            term = contract(xbuf[0, rows, pl.ds(r0, r_n)], ybuf[0, rows, pl.ds(c0, c_n)])
            part[at] = term if c == 0 else part[at] + term
        if j == 0:
            pl.semaphore_wait(barrier, plane)
        first_part(other, j).start()
    w_copies = [pltpu.make_async_copy(w_refs[i], w_outs[i], w_sem.at[i]) for i in range(4)]

    def tiles(lo, hi):
        @pl.loop(lo, hi)
        def _(s):
            tile, slot = tile_of(s), slot_of(s)

            @pl.when(s + 1 < n_steps)
            def _():
                load(s + 1)

            for h in range(HALVES):
                load_done(slot, h)
                rows = pl.ds(h * half, half)
                term = contract(xbuf[slot, rows, :], ybuf[slot, rows, :])
                if h == 0:
                    part[tile] = term
                else:
                    part[tile] += term

            @pl.when(s != 1)
            def _():
                bulk(tile).start()

    beta_two, rho_step, clip_thr = hyper[0], hyper[1], hyper[2]

    def w_at(i, t, r):
        if geo.wide(i):
            return pl.ds(r, RB), pl.ds(pl.multiple_of(t * TN, TN), TN)
        return pl.ds(t * TM + r, RB), pl.ds(0, TN)

    def stat_at(i, t, r):
        return pl.ds(r, RB) if geo.wide(i) else pl.ds(t * TM + r, RB)

    def stat_tile(i, t, rows_ref, accumulate, col_sum):
        tile = geo.mats[i][0] + t

        def step(b, acc):
            r = pl.multiple_of(b * RB, RB)
            grad = part[tile, pl.ds(r, RB), :] + peer[tile, pl.ds(r, RB), :]
            peer[tile, pl.ds(r, RB), :] = grad
            sq = grad * grad + EPS_ONE
            at = stat_at(i, t, r)
            if accumulate:
                rows_ref[at, :] += fold_lanes(sq)
            else:
                rows_ref[at, :] = fold_lanes(sq)
            return acc + fold_rows(sq)

        return lax.fori_loop(0, TM // RB, step, col_sum)

    def norm_tile(i, t, acc):
        tile = geo.mats[i][0] + t
        scale = brow[:, pl.ds(pl.multiple_of(t * TN, TN), TN)] if geo.wide(i) else brow[:, pl.ds(0, TN)]

        def step(b, acc):
            r = pl.multiple_of(b * RB, RB)
            upd = peer[tile, pl.ds(r, RB), :] * scale
            lane_scale = acol[stat_at(i, t, r), :]
            return acc + fold_rows(fold_lanes(upd * upd) * lane_scale * lane_scale)

        return lax.fori_loop(0, TM // RB, step, acc)

    def write_tile(i, t, step_size):
        tile = geo.mats[i][0] + t
        scale = brow[:, pl.ds(pl.multiple_of(t * TN, TN), TN)] if geo.wide(i) else brow[:, pl.ds(0, TN)]
        scale = scale * step_size

        def step(b, _):
            r = pl.multiple_of(b * RB, RB)
            upd = peer[tile, pl.ds(r, RB), :] * scale
            lane_scale = jnp.concatenate([acol[stat_at(i, t, r), :]] * (TN // LANES), axis=1)
            w_outs[i][w_at(i, t, r)] = w_outs[i][w_at(i, t, r)] - upd * lane_scale
            return 0

        lax.fori_loop(0, TM // RB, step, 0)

    def weight_squares(i):
        acc = jnp.zeros((8, LANES), F32)
        for t in range(geo.mats[i][1]):
            def step(b, acc):
                w = w_outs[i][w_at(i, t, pl.multiple_of(b * RB, RB))]
                return acc + fold_rows(fold_lanes(w * w))

            acc = lax.fori_loop(0, TM // RB, step, acc)
        w_sq[pl.ds(i, 1), :] = row_sum_of(acc)

    def row_totals(rows_ref, j):
        return row_sum_of(jnp.transpose(rows_ref[pl.ds(j, LANES), :]))

    def exchange(i, buf, send, recv):
        copies = []
        for step in range(1, plane):
            device = plane_peer(step)[1]
            copies.append(remote(buf.at[me], buf.at[me], send.at[i, step], recv.at[i, me], device))
        for copy in copies:
            copy.start()
        for step in range(1, plane):
            there, device = plane_peer(step)
            remote(buf.at[there], buf.at[there], send.at[i, step], recv.at[i, there], device).wait_recv()
        return copies

    def sizes(i):
        _, _, m_loc, n_loc = geo.mats[i]
        return m_loc, n_loc, m_loc + n_loc, m_loc * n_row, n_loc * n_col

    def round_one(i, z_part):
        m_loc, n_loc, tail, m_total, n_total = sizes(i)
        one = msg_one[i]
        r_fold = jnp.zeros((1, LANES), F32)
        for j in range(0, m_loc, LANES):
            total = row_totals(rowpart, j)
            if z_part:
                total = total + (zmsg_one[0, :, pl.ds(j, LANES)] + zmsg_one[1, :, pl.ds(j, LANES)])
            one[pl.ds(me, 1), :, pl.ds(j, LANES)] = total[None]
            r_fold = r_fold + r_refs[i][:, pl.ds(j, LANES)]
        one[pl.ds(me, 1), :, pl.ds(m_loc, n_loc)] = colpart[:, pl.ds(0, n_loc)][None]
        if z_part:
            for t in range(2):
                one[pl.ds(me, 1), :, pl.ds(m_loc + t * TN, TN)] = zmsg_one[t, :, pl.ds(m_loc, TN)][None]
        one[pl.ds(me, 1), :, pl.ds(tail, LANES)] = r_fold[None]
        one[pl.ds(me, 1), :, pl.ds(tail + LANES, LANES)] = w_sq[pl.ds(i, 1), :][None]
        sent = exchange(i, one, one_send, one_recv)

        row_sum = one[row, :, pl.ds(0, m_loc)]
        for j in range(1, n_col):
            row_sum = row_sum + one[j * n_row + row, :, pl.ds(0, m_loc)]
        col_sum = one[col * n_row, :, pl.ds(m_loc, n_loc)]
        for j in range(1, n_row):
            col_sum = col_sum + one[col * n_row + j, :, pl.ds(m_loc, n_loc)]
        new_row = beta_two * r_refs[i][...] + (1.0 - beta_two) * (row_sum / n_total)
        new_col = beta_two * c_refs[i][...] + (1.0 - beta_two) * (col_sum / m_total)
        r_outs[i][...] = new_row
        c_outs[i][...] = new_col

        old_fold = jnp.zeros((1, LANES), F32)
        sq_fold = jnp.zeros((1, LANES), F32)
        for j in range(plane):
            sq_fold = sq_fold + fold_lanes(one[j, :, pl.ds(0, m_loc)])
            if j < n_row:
                old_fold = old_fold + one[j, :, pl.ds(tail, LANES)]
        total = lane_sum(beta_two * old_fold + (1.0 - beta_two) * (sq_fold / n_total))

        row_scale = 1.0 / jnp.sqrt(new_row / total)
        for j in range(0, m_loc, LANES):
            acol[pl.ds(j, LANES), :] = jnp.transpose(jnp.broadcast_to(row_scale[:, j:j + LANES], (LANES, LANES)))
        brow[:, pl.ds(0, n_loc)] = 1.0 / jnp.sqrt(new_col)
        return sent

    def round_two(i, upd_sq):
        _, _, tail, m_total, n_total = sizes(i)
        one, two = msg_one[i], msg_two.at[i]
        two[pl.ds(me, 1)] = upd_sq[None]
        sent = exchange(i, two, two_send, two_recv)
        upd_fold, w_fold = two[0], one[0, :, pl.ds(tail + LANES, LANES)]
        for j in range(1, plane):
            upd_fold = upd_fold + two[j]
            w_fold = w_fold + one[j, :, pl.ds(tail + LANES, LANES)]
        upd_rms = jnp.sqrt(lane_sum(upd_fold) / (m_total * n_total))
        w_rms = jnp.sqrt(lane_sum(w_fold) / (m_total * n_total))
        return rho_step * jnp.maximum(EPS_TWO, w_rms) / jnp.maximum(1.0, upd_rms / clip_thr), sent

    none = jnp.zeros((8, TN), F32)
    no_lanes = jnp.zeros((8, LANES), F32)
    m_gate = geo.mats[0][2]

    tiles(0, 4)

    for copy in w_copies:
        copy.start()
    for copy in w_copies:
        copy.wait()
    for i in range(4):
        weight_squares(i)
    for j in range(len(PARTS)):
        first_part(own, j).wait_recv()
    own_col = stat_tile(0, own, rowpart_own, False, none)
    for j in range(0, TM, LANES):
        zmsg_one[pl.ds(own, 1), :, pl.ds(j, LANES)] = row_totals(rowpart_own, j)[None]
    zmsg_one[pl.ds(own, 1), :, pl.ds(m_gate, TN)] = row_sum_of(own_col)[None]
    z_copy(0, zmsg_one, own).start()

    tiles(4, 6)

    shared = range(2, geo.mats[0][1])
    for t in shared:
        bulk(t).wait_recv()
        colpart[:, pl.ds(t * TN, TN)] = row_sum_of(stat_tile(0, t, rowpart, t > 2, none))
    z_copy(0, zmsg_one, other).wait_recv()
    gate_sent = round_one(0, True)
    zmsg_two[pl.ds(own, 1)] = row_sum_of(norm_tile(0, own, no_lanes))[None]
    z_copy(1, zmsg_two, own).start()

    tiles(6, 8)

    upd_sq = no_lanes
    for t in shared:
        upd_sq = norm_tile(0, t, upd_sq)
    z_copy(1, zmsg_two, other).wait_recv()
    step_size, sent = round_two(0, row_sum_of(upd_sq) + (zmsg_two[0] + zmsg_two[1]))
    gate_sent += sent
    write_tile(0, own, step_size)
    for t in shared:
        write_tile(0, t, step_size)

    tiles(8, geo.n_tiles - 1)
    gather(own).start()

    for i in range(1, 4):
        first, count, m_loc, n_loc = geo.mats[i]
        col_sum = none
        for t in range(count):
            bulk(first + t).wait_recv()
            if geo.wide(i):
                colpart[:, pl.ds(t * TN, TN)] = row_sum_of(stat_tile(i, t, rowpart, t > 0, none))
            else:
                col_sum = stat_tile(i, t, rowpart, False, col_sum)
        if not geo.wide(i):
            colpart[:, pl.ds(0, TN)] = row_sum_of(col_sum)
        sent_one = round_one(i, False)
        upd_sq = no_lanes
        for t in range(count):
            upd_sq = norm_tile(i, t, upd_sq)
        step_size, sent_two = round_two(i, row_sum_of(upd_sq))
        for t in range(count):
            write_tile(i, t, step_size)
        for copy in sent_one + sent_two:
            copy.wait_send()

    for copy in gate_sent:
        copy.wait_send()
    z_copy(0, zmsg_one, own).wait_send()
    z_copy(1, zmsg_two, own).wait_send()
    for j in range(len(PARTS)):
        first_part(other, j).wait_send()

    @pl.loop(2, geo.n_tiles)
    def _(tile):
        bulk(tile).wait_send()

    gather(own).wait_send()
    gather(other).wait_recv()


def write_out(*refs):
    copies = [pltpu.make_async_copy(refs[i], refs[12 + i], refs[24].at[i]) for i in range(12)]
    for copy in copies:
        copy.start()
    for copy in copies:
        copy.wait()


class Geometry:
    def __init__(self, n_row, n_col, tokens, blocks):
        self.n_row, self.n_col = n_row, n_col
        self.tokens = tokens
        self.mats, first = [], 0
        for m_loc, n_loc in blocks:
            count = (m_loc // TM) * (n_loc // TN)
            self.mats.append((first, count, m_loc, n_loc))
            first += count
        self.n_tiles = first

    def wide(self, i):
        return self.mats[i][2] == TM

    def groups(self, x_refs, dy_refs):
        for (first, count, m_loc, _), x_ref, y_ref in zip(self.mats, x_refs, dy_refs):
            yield first, count, m_loc // TM, x_ref, y_ref


def solution(mesh):
    n_row, n_col = mesh.shape["row"], mesh.shape["col"]
    plane = n_row * n_col
    act_spec = P('dp', 'row')
    grad_spec = P('dp', 'col')
    w_spec = P('row', 'col')
    row_spec = P('row')
    col_spec = P('col')
    in_specs = (act_spec, grad_spec, act_spec, grad_spec, grad_spec, act_spec, grad_spec,
                w_spec, w_spec, w_spec, w_spec,
                row_spec, col_spec, row_spec, col_spec, row_spec, col_spec, row_spec, col_spec, P())
    out_specs = (w_spec, row_spec, col_spec) * 4

    def per_device(x_attn, dy_attn, x_mlp, dy_gate, dy_up, h_mlp, dy_out, w_attn, w_gate, w_up, w_down,
                   r_attn, c_attn, r_gate, c_gate, r_up, c_up, r_down, c_down, hyper_params):
        weights = (w_gate, w_up, w_down, w_attn)
        rows = [v.reshape(1, -1) for v in (r_gate, r_up, r_down, r_attn)]
        cols = [v.reshape(1, -1) for v in (c_gate, c_up, c_down, c_attn)]
        blocks = [w.shape for w in weights]
        geo = Geometry(n_row, n_col, x_attn.shape[0], blocks)
        results = (*weights, *rows, *cols)
        hbm = pl.BlockSpec(memory_space=pl.ANY)
        vmem = pl.BlockSpec(memory_space=pltpu.VMEM)
        smem = pl.BlockSpec(memory_space=pltpu.SMEM)
        dma = pltpu.SemaphoreType.DMA
        max_m, max_n = max(b[0] for b in blocks), max(b[1] for b in blocks)

        def body(*refs):
            xs = (refs[0], refs[0], refs[1], refs[2])
            kernel(geo, xs, refs[3:7], refs[7:11], refs[11:15], refs[15:19], refs[19],
                   refs[20:24], refs[24:28], refs[28:32],
                   *refs[32:42], refs[42:46], *refs[46:])

        outs = pl.pallas_call(
            body,
            out_shape=tuple(pltpu.VMEM(v.shape, F32) for v in results),
            in_specs=[hbm] * 11 + [vmem] * 8 + [smem],
            out_specs=(vmem,) * 12,
            scratch_shapes=[
                pltpu.VMEM((2, geo.tokens, TM), jnp.bfloat16),
                pltpu.VMEM((2, geo.tokens, TN), jnp.bfloat16),
                pltpu.VMEM((geo.n_tiles, TM, TN), F32),
                pltpu.VMEM((geo.n_tiles, TM, TN), F32),
                pltpu.VMEM((max_m, LANES), F32),
                pltpu.VMEM((TM, LANES), F32),
                pltpu.VMEM((max_m, LANES), F32),
                pltpu.VMEM((1, max_n), F32),
                pltpu.VMEM((1, max_n), F32),
                pltpu.VMEM((8, LANES), F32),
            ] + [pltpu.VMEM((plane, 1, m + n + 2 * LANES), F32) for m, n in blocks] + [
                pltpu.VMEM((4, plane, 1, LANES), F32),
                pltpu.VMEM((2, 1, TM + TN), F32),
                pltpu.VMEM((2, 1, LANES), F32),
                dma((2, HALVES)), dma((2, HALVES)), dma((5, 4)), dma((4,)),
                dma((len(PARTS),)), dma((len(PARTS),)), dma((geo.n_tiles,)), dma((geo.n_tiles,)), dma((2,)),
                dma((4, plane)), dma((4, plane)), dma((4, plane)), dma((4, plane)), dma((2,)), dma((2,)),
            ],
            compiler_params=pltpu.CompilerParams(
                collective_id=0, has_side_effects=True, vmem_limit_bytes=48 << 20),
            name="adafactor_step",
        )(x_mlp, h_mlp, x_attn, dy_gate, dy_up, dy_out, dy_attn, *weights, *rows, *cols, hyper_params)
        outs = pl.pallas_call(
            write_out,
            out_shape=tuple(jax.ShapeDtypeStruct(v.shape, F32) for v in results),
            in_specs=[vmem] * 12,
            out_specs=(hbm,) * 12,
            scratch_shapes=[dma((12,))],
            compiler_params=pltpu.CompilerParams(vmem_limit_bytes=1 << 20),
            name="write_out",
        )(*[pltpu.with_memory_space_constraint(v, pltpu.VMEM) for v in outs])
        w_new, r_new, c_new = outs[:4], outs[4:8], outs[8:]
        result = []
        for i in (3, 0, 1, 2):
            result += [w_new[i], r_new[i].reshape(-1), c_new[i].reshape(-1)]
        return tuple(result)

    return jax.shard_map(per_device, mesh=mesh, in_specs=in_specs, out_specs=out_specs, check_vma=False)
```

time: 169 us -> 160 us (0.947)
  Pallas kernels: 168 us -> 159 us
    pallas_call x1, Pallas kernels: 165 us -> 156 us  [per_device(): pl.pallas_call(body, out_shape=tuple((pltpu.VMEM(v.shape, F32) for v in r...]
where the time goes in v3:
time: 160 us
  Pallas kernels  159 us (99%)
    pallas_call x1, Pallas kernels, per_device(): pl.pallas_call(body, out_shape=tuple((pltpu.VMEM(v.shape, F32) for v in r...  156 us

profile of v3, /device:TPU:0, one launch (start us, length us, event | category | flops | bytes accessed | tf_op | source)
XLA Modules:
  0.0 160.0 jit_solution(11533264283687320967)
XLA Ops:
  0.7 156.3 %adafactor_step.1 = (f32[256,2048]{1,0:T(8,128)S(1)}, f32[256,2048]{1,0:T(8,128)S(1)}, f32[1024,512]{1,0:T(8,128)S(1)}, f32[256,512]{1,0:T(8,128)S(1)}, f32[1,25...) custom-call(bf16[8192,256]{1,0:T(8,128)(2,1)} %refs_0_.1, ...), custom_call_target="tpu_custom_call" | custom-call | tf_op jit(solution)/shard_map/adafactor_step/pallas_call | solution.py:456
  156.9 2.9 %write_out.1 = (f32[256,2048]{1,0:T(8,128)}, f32[256,2048]{1,0:T(8,128)}, f32[1024,512]{1,0:T(8,128)}, f32[256,512]{1,0:T(8,128)}, f32[1,256]{1,0:T(1,128)}, /*i...) custom-call(f32[256,2048]{1,0:T(8,128)S(1)} %get-tuple-element.36.re, ...), custom_call_target="tpu_custom_call" | custom-call | tf_op jit(solution)/shard_map/write_out/pallas_call | solution.py:484

commit v4 on v3

--- a/solution.py
+++ b/solution.py
@@ -39,16 +39,18 @@
     return jnp.sum(v, axis=0, keepdims=True)
 
 
-def kernel(geo, x_refs, dy_refs, w_refs, r_refs, c_refs, hyper, w_outs, r_outs, c_outs,
+def kernel(geo, x_refs, dy_refs, w_refs, small_refs, w_outs, r_outs, c_outs, small,
            xbuf, ybuf, part, peer, rowpart, rowpart_own, acol, brow, colpart, w_sq, msg_one, msg_two, zmsg_one, zmsg_two,
            x_sem, y_sem, first_sem, w_sem, sub_send, sub_recv, bulk_send, bulk_recv, gather_sem,
-           one_send, one_recv, two_send, two_recv, z_send, z_recv):
+           one_send, one_recv, two_send, two_recv, z_send, z_recv, small_sem, near_sem):
+    r_refs, c_refs, hyper = small[:4], small[4:8], small[8]
     n_col, n_row = geo.n_col, geo.n_row
     plane = n_col * n_row
     dp, col, row = lax.axis_index("dp"), lax.axis_index("col"), lax.axis_index("row")
     me = col * n_row + row
     own, other = dp, 1 - dp
     across = (1 - dp, col, row)
+    near = ((dp, col, row + 1 - 2 * lax.rem(row, 2)), (dp, col, lax.rem(row + n_row // 2, n_row)), (dp, lax.rem(col + 1, n_col), row))
 
     def plane_peer(step):
         other = lax.rem(me + step, plane)
@@ -133,9 +135,8 @@
     load(0)
 
     barrier = pltpu.get_barrier_semaphore()
-    for step in range(1, plane):
-        pl.semaphore_signal(barrier, inc=1, device_id=plane_peer(step)[1], device_id_type=MESH)
-    pl.semaphore_signal(barrier, inc=1, device_id=across, device_id_type=MESH)
+    for device in (across, *near):
+        pl.semaphore_signal(barrier, inc=1, device_id=device, device_id_type=MESH)
 
     for j, (pieces, copies_of) in enumerate(first_loads):
         r0, r_n, c0, c_n = PARTS[j]
@@ -147,9 +148,10 @@
             term = contract(xbuf[0, rows, pl.ds(r0, r_n)], ybuf[0, rows, pl.ds(c0, c_n)])
             part[at] = term if c == 0 else part[at] + term
         if j == 0:
-            pl.semaphore_wait(barrier, plane)
+            pl.semaphore_wait(barrier, 1 + len(near))
         first_part(other, j).start()
     w_copies = [pltpu.make_async_copy(w_refs[i], w_outs[i], w_sem.at[i]) for i in range(4)]
+    w_copies += [pltpu.make_async_copy(a, b, small_sem.at[i]) for i, (a, b) in enumerate(zip(small_refs, small))]
 
     def tiles(lo, hi):
         @pl.loop(lo, hi)
@@ -172,8 +174,6 @@
             @pl.when(s != 1)
             def _():
                 bulk(tile).start()
-
-    beta_two, rho_step, clip_thr = hyper[0], hyper[1], hyper[2]
 
     def w_at(i, t, r):
         if geo.wide(i):
@@ -319,8 +319,15 @@
 
     for copy in w_copies:
         copy.start()
+
+    for n in range(2):
+        for device in near:
+            pl.semaphore_signal(near_sem.at[n], inc=1, device_id=device, device_id_type=MESH)
+        pl.semaphore_wait(near_sem.at[n], len(near))
+
     for copy in w_copies:
         copy.wait()
+    beta_two, rho_step, clip_thr = hyper[0], hyper[1], hyper[2]
     for i in range(4):
         weight_squares(i)
     for j in range(len(PARTS)):
@@ -443,22 +450,21 @@
         results = (*weights, *rows, *cols)
         hbm = pl.BlockSpec(memory_space=pl.ANY)
         vmem = pl.BlockSpec(memory_space=pltpu.VMEM)
-        smem = pl.BlockSpec(memory_space=pltpu.SMEM)
         dma = pltpu.SemaphoreType.DMA
         max_m, max_n = max(b[0] for b in blocks), max(b[1] for b in blocks)
 
         def body(*refs):
             xs = (refs[0], refs[0], refs[1], refs[2])
-            kernel(geo, xs, refs[3:7], refs[7:11], refs[11:15], refs[15:19], refs[19],
-                   refs[20:24], refs[24:28], refs[28:32],
-                   *refs[32:42], refs[42:46], *refs[46:])
+            kernel(geo, xs, refs[3:7], refs[7:11], refs[11:20], refs[20:24], refs[24:28], refs[28:32], refs[32:41],
+                   *refs[41:51], refs[51:55], *refs[55:])
 
         outs = pl.pallas_call(
             body,
             out_shape=tuple(pltpu.VMEM(v.shape, F32) for v in results),
-            in_specs=[hbm] * 11 + [vmem] * 8 + [smem],
+            in_specs=[hbm] * 20,
             out_specs=(vmem,) * 12,
-            scratch_shapes=[
+            scratch_shapes=[pltpu.VMEM(v.shape, F32) for v in (*rows, *cols)] + [
+                pltpu.SMEM((3,), F32),
                 pltpu.VMEM((2, geo.tokens, TM), jnp.bfloat16),
                 pltpu.VMEM((2, geo.tokens, TN), jnp.bfloat16),
                 pltpu.VMEM((geo.n_tiles, TM, TN), F32),
@@ -475,7 +481,8 @@
                 pltpu.VMEM((2, 1, LANES), F32),
                 dma((2, HALVES)), dma((2, HALVES)), dma((5, 4)), dma((4,)),
                 dma((len(PARTS),)), dma((len(PARTS),)), dma((geo.n_tiles,)), dma((geo.n_tiles,)), dma((2,)),
-                dma((4, plane)), dma((4, plane)), dma((4, plane)), dma((4, plane)), dma((2,)), dma((2,)),
+                dma((4, plane)), dma((4, plane)), dma((4, plane)), dma((4, plane)), dma((2,)), dma((2,)), dma((9,)),
+                pltpu.SemaphoreType.REGULAR((2,)),
             ],
             compiler_params=pltpu.CompilerParams(
                 collective_id=0, has_side_effects=True, vmem_limit_bytes=48 << 20),

time: 160 us -> 159 us (level)
  no operation moved by 1% of the time
where the time goes in v4:
time: 159 us
  Pallas kernels  158 us (99%)
    pallas_call x1, Pallas kernels, per_device(): pl.pallas_call(body, out_shape=tuple((pltpu.VMEM(v.shape, F32) for v in r...  155 us

profile of v4, /device:TPU:0, one launch (start us, length us, event | category | flops | bytes accessed | tf_op | source)
XLA Modules:
  0.0 159.1 jit_solution(13941158242332843281)
XLA Ops:
  0.7 155.4 %adafactor_step.1 = (f32[256,2048]{1,0:T(8,128)S(1)}, f32[256,2048]{1,0:T(8,128)S(1)}, f32[1024,512]{1,0:T(8,128)S(1)}, f32[256,512]{1,0:T(8,128)S(1)}, f32[1,25...) custom-call(bf16[8192,256]{1,0:T(8,128)(2,1)} %refs_0_.1, ...), custom_call_target="tpu_custom_call" | custom-call | tf_op jit(solution)/shard_map/adafactor_step/pallas_call | solution.py:461
  156.0 2.9 %write_out.1 = (f32[256,2048]{1,0:T(8,128)}, f32[256,2048]{1,0:T(8,128)}, f32[1024,512]{1,0:T(8,128)}, f32[256,512]{1,0:T(8,128)}, f32[1,256]{1,0:T(1,128)}, /*i...) custom-call(f32[256,2048]{1,0:T(8,128)S(1)} %get-tuple-element.36.re, ...), custom_call_target="tpu_custom_call" | custom-call | tf_op jit(solution)/shard_map/write_out/pallas_call | solution.py:491

commit v5 on v4

--- a/solution.py
+++ b/solution.py
@@ -12,7 +12,7 @@
 
 TM, TN = 256, 512
 HALVES = 2
-PARTS = ((0, 128, 0, 128), (128, 128, 0, 128), (0, 256, 128, 128), (0, 256, 256, 256))
+PARTS = ((0, 128, 0, 128), (0, 128, 128, 128), (128, 128, 0, 256), (0, 256, 256, 256))
 RB = 32
 LANES = 128
 
@@ -74,6 +74,10 @@
 
     def z_copy(n, buf, slot):
         return remote(buf.at[slot], buf.at[slot], z_send.at[n], z_recv.at[n], across)
+
+    barrier = pltpu.get_barrier_semaphore()
+    for device in (across, *near):
+        pl.semaphore_signal(barrier, inc=1, device_id=device, device_id_type=MESH)
 
     half = geo.tokens // HALVES
 
@@ -124,19 +128,19 @@
 
     first_loads = (
         (4, lambda c: (first_x(0, 4, c, 0, 128), first_y(1, 4, c, 0, 128))),
-        (2, lambda c: (first_x(2, 2, c, 128, 128),)),
-        (2, lambda c: (first_y(3, 2, c, 128, 128),)),
+        (2, lambda c: (first_y(2, 2, c, 128, 128),)),
+        (2, lambda c: (first_x(3, 2, c, 128, 128),)),
         (2, lambda c: (first_y(4, 2, c, 256, 256),)),
     )
-    for pieces, copies_of in first_loads:
+    def start_first(j):
+        pieces, copies_of = first_loads[j]
         for c in range(pieces):
             for copy in copies_of(c):
                 copy.start()
-    load(0)
-
-    barrier = pltpu.get_barrier_semaphore()
-    for device in (across, *near):
-        pl.semaphore_signal(barrier, inc=1, device_id=device, device_id_type=MESH)
+
+    for j in range(4):
+        start_first(j)
+    starts = {(2, 0): lambda: load(0)}
 
     for j, (pieces, copies_of) in enumerate(first_loads):
         r0, r_n, c0, c_n = PARTS[j]
@@ -144,12 +148,24 @@
         for c in range(pieces):
             for copy in copies_of(c):
                 copy.wait()
+            if (j, c) in starts:
+                starts[j, c]()
             rows = pl.ds(c * (geo.tokens // pieces), geo.tokens // pieces)
             term = contract(xbuf[0, rows, pl.ds(r0, r_n)], ybuf[0, rows, pl.ds(c0, c_n)])
             part[at] = term if c == 0 else part[at] + term
         if j == 0:
             pl.semaphore_wait(barrier, 1 + len(near))
-        first_part(other, j).start()
+        if j in (2,):
+            @pl.when(lax.rem(row, 2) == 0)
+            def _():
+                first_part(other, j).start()
+        else:
+            if j == 3:
+                @pl.when(lax.rem(row, 2) == 1)
+                def _():
+                    for held in (2,):
+                        first_part(other, held).start()
+            first_part(other, j).start()
     w_copies = [pltpu.make_async_copy(w_refs[i], w_outs[i], w_sem.at[i]) for i in range(4)]
     w_copies += [pltpu.make_async_copy(a, b, small_sem.at[i]) for i, (a, b) in enumerate(zip(small_refs, small))]
 

time: 159 us -> 158 us (level)
  no operation moved by 1% of the time
where the time goes in v5:
time: 158 us
  Pallas kernels  157 us (99%)
    pallas_call x1, Pallas kernels, per_device(): pl.pallas_call(body, out_shape=tuple((pltpu.VMEM(v.shape, F32) for v in r...  154 us

profile of v5, /device:TPU:0, one launch (start us, length us, event | category | flops | bytes accessed | tf_op | source)
XLA Modules:
  0.0 158.0 jit_solution(8967287694922697693)
XLA Ops:
  0.7 154.2 %adafactor_step.1 = (f32[256,2048]{1,0:T(8,128)S(1)}, f32[256,2048]{1,0:T(8,128)S(1)}, f32[1024,512]{1,0:T(8,128)S(1)}, f32[256,512]{1,0:T(8,128)S(1)}, f32[1,25...) custom-call(bf16[8192,256]{1,0:T(8,128)(2,1)} %refs_0_.1, ...), custom_call_target="tpu_custom_call" | custom-call | tf_op jit(solution)/shard_map/adafactor_step/pallas_call | solution.py:477
  154.9 2.9 %write_out.1 = (f32[256,2048]{1,0:T(8,128)}, f32[256,2048]{1,0:T(8,128)}, f32[1024,512]{1,0:T(8,128)}, f32[256,512]{1,0:T(8,128)}, f32[1,256]{1,0:T(1,128)}, /*i...) custom-call(f32[256,2048]{1,0:T(8,128)S(1)} %get-tuple-element.36.re, ...), custom_call_target="tpu_custom_call" | custom-call | tf_op jit(solution)/shard_map/write_out/pallas_call | solution.py:507

commit v6 on v5

--- a/solution.py
+++ b/solution.py
@@ -74,10 +74,6 @@
 
     def z_copy(n, buf, slot):
         return remote(buf.at[slot], buf.at[slot], z_send.at[n], z_recv.at[n], across)
-
-    barrier = pltpu.get_barrier_semaphore()
-    for device in (across, *near):
-        pl.semaphore_signal(barrier, inc=1, device_id=device, device_id_type=MESH)
 
     half = geo.tokens // HALVES
 
@@ -141,6 +137,11 @@
     for j in range(4):
         start_first(j)
     starts = {(2, 0): lambda: load(0)}
+
+    barrier = pltpu.get_barrier_semaphore()
+    for device in (across, *near):
+        pl.semaphore_signal(barrier, inc=1, device_id=device, device_id_type=MESH)
+
 
     for j, (pieces, copies_of) in enumerate(first_loads):
         r0, r_n, c0, c_n = PARTS[j]
@@ -308,7 +309,7 @@
                 old_fold = old_fold + one[j, :, pl.ds(tail, LANES)]
         total = lane_sum(beta_two * old_fold + (1.0 - beta_two) * (sq_fold / n_total))
 
-        row_scale = 1.0 / jnp.sqrt(new_row / total)
+        row_scale = jnp.sqrt(total) / jnp.sqrt(new_row)
         for j in range(0, m_loc, LANES):
             acol[pl.ds(j, LANES), :] = jnp.transpose(jnp.broadcast_to(row_scale[:, j:j + LANES], (LANES, LANES)))
         brow[:, pl.ds(0, n_loc)] = 1.0 / jnp.sqrt(new_col)

time: 158 us -> 158 us (level)
  no operation moved by 1% of the time
where the time goes in v6:
time: 158 us
  Pallas kernels  157 us (99%)
    pallas_call x1, Pallas kernels, per_device(): pl.pallas_call(body, out_shape=tuple((pltpu.VMEM(v.shape, F32) for v in r...  154 us

profile of v6, /device:TPU:0, one launch (start us, length us, event | category | flops | bytes accessed | tf_op | source)
XLA Modules:
  0.0 157.9 jit_solution(304242029790957688)
XLA Ops:
  0.7 154.2 %adafactor_step.1 = (f32[256,2048]{1,0:T(8,128)S(1)}, f32[256,2048]{1,0:T(8,128)S(1)}, f32[1024,512]{1,0:T(8,128)S(1)}, f32[256,512]{1,0:T(8,128)S(1)}, f32[1,25...) custom-call(bf16[8192,256]{1,0:T(8,128)(2,1)} %refs_0_.1, ...), custom_call_target="tpu_custom_call" | custom-call | tf_op jit(solution)/shard_map/adafactor_step/pallas_call | solution.py:478
  154.8 2.9 %write_out.1 = (f32[256,2048]{1,0:T(8,128)}, f32[256,2048]{1,0:T(8,128)}, f32[1024,512]{1,0:T(8,128)}, f32[256,512]{1,0:T(8,128)}, f32[1,256]{1,0:T(1,128)}, /*i...) custom-call(f32[256,2048]{1,0:T(8,128)S(1)} %get-tuple-element.36.re, ...), custom_call_target="tpu_custom_call" | custom-call | tf_op jit(solution)/shard_map/write_out/pallas_call | solution.py:508
